TPU v7x, 32 devices: a whole 2x2x4 slice. The times are simulated.
32 devices in a mesh: grp: 2 (over x), dap: 16 (over z, y, core).
Axes of the slice: x: 2, y: 2, z: 4, core: 2. Of those that a mesh axis runs over, the one named last changes fastest.
Arguments:
- homolog_stack_tensor: bfloat16 [64, 64, 256], P(('grp', 'dap')), parts along dimension 0, may hold values from -6.5 to 6.5
- occupancy_indicator: int32 [64, 64], P('grp'), parts along dimension 0, may hold values from 0 to 1, as said below
- chain_existence_flags: int32 [64], P('grp'), parts along dimension 0, may hold values from 0 to 1, as said below
- focus_normal_factor: float32 [256], replicated, may hold values from 0.25 to 1.75
- focus_normal_addend: float32 [256], replicated, may hold values from -3 to 3
- probe_index_weights: bfloat16 [256, 512], replicated, may hold values from -3 to 3
- payload_valve_weights: bfloat16 [256, 512], replicated, may hold values from -0.375 to 0.375
- logistic_valve_addend: float32 [256], replicated, may hold values from -4 to 4
- focus_exit_weights: bfloat16 [256, 256], replicated, may hold values from -0.375 to 0.375
- focus_exit_addend: float32 [256], replicated, may hold values from -3 to 3
- product_mean_layer_stretch: float32 [256], replicated, may hold values from 0.25 to 1.75
- product_mean_layer_shift: float32 [256], replicated, may hold values from -2 to 2
- twin_map_matrix: bfloat16 [256, 64], replicated, may hold values from -0.375 to 0.375
- twin_map_shift: float32 [64], replicated, may hold values from -2 to 2
- couple_map_matrix: bfloat16 [1024, 128], replicated, may hold values from -0.75 to 0.75
- couple_map_shift: float32 [128], replicated, may hold values from -3 to 3
Outputs:
- alignment_after: bfloat16 [64, 64, 256], P('grp', 'dap'), parts along dimension 0
- pair_features_after: bfloat16 [128, 64, 128], P(('grp', 'dap')), parts along dimension 0
There are 2 independent parts, one for each index of `grp`. A program takes and returns all parts, laid end to end along the dimension named above; an argument that names none is the same for every part. Nothing has to cross between parts.
Inputs may be any that keep to these rules, and one draw needn't show every extreme that they name: `chain_existence_flags`: 1 for the first 16 sequences, 0 for the last one. `occupancy_indicator`: every sequence is 0 from some residue on (the last residue always, never more than the last 32); before it sequence 0 is all 1 and the others have gaps.
All inputs are finite; a program needn't handle non-finite values.
Results may differ from a plain program's by a relative error of at most 0.008.
Values may be sent and summed in bfloat16 or wider, within the bound.
No kernel may reach another device: no remote copies, remote signals or barrier semaphores. Data moves between devices by JAX's collectives and lax.ppermute only.
A program may use at most 64 MiB of HBM per device.

v0:
```python
import jax
import jax.numpy as jnp
from jax import lax
from jax.sharding import PartitionSpec as P

HEAD_COUNT = 8
HEAD_CHANNELS = 32
OUTER_CHANNELS = 32
PAIR_DIM = 128


EPSILON = 1e-05
MASKED = -100000.0


def layer_norm(value_vectors, scale_vec, shift_vec):
    widened = value_vectors.astype(jnp.float32)
    centred = widened - jnp.mean(widened, axis=-1, keepdims=True)
    variance = jnp.mean(centred * centred, axis=-1, keepdims=True)
    scaled = centred * lax.rsqrt(variance + EPSILON)
    return (scaled * scale_vec + shift_vec).astype(jnp.bfloat16)


def heed_across_lanes(
    vertical_pieces,
    present_mask,
    focus_normal_factor,
    focus_normal_addend,
    probe_index_weights,
    payload_valve_weights,
    logistic_valve_addend,
    focus_exit_weights,
    focus_exit_addend,
):
    seq_count, res_count, feature_width = vertical_pieces.shape
    inner_channel_width = HEAD_COUNT * HEAD_CHANNELS
    normed = layer_norm(vertical_pieces, focus_normal_factor, focus_normal_addend).reshape(
        seq_count * res_count, feature_width
    )
    query_key = jnp.dot(normed, probe_index_weights, preferred_element_type=jnp.float32)
    value_gate = jnp.dot(normed, payload_valve_weights, preferred_element_type=jnp.float32)
    head_shape = (seq_count, res_count, HEAD_COUNT, HEAD_CHANNELS)
    query_rows_all = (
        (query_key[:, :inner_channel_width] * HEAD_CHANNELS ** (-0.5))
        .astype(jnp.bfloat16)
        .reshape(head_shape)
    )
    key_rows = query_key[:, inner_channel_width:].astype(jnp.bfloat16).reshape(head_shape)
    value_rows = value_gate[:, :inner_channel_width].astype(jnp.bfloat16).reshape(head_shape)
    gating = jax.nn.sigmoid(value_gate[:, inner_channel_width:] + logistic_valve_addend)
    scores = jnp.einsum(
        "srhd,trhd->rhst", query_rows_all, key_rows, preferred_element_type=jnp.float32
    )
    allowed = jnp.transpose(present_mask > 0)[:, None, None, :]
    scores = jnp.where(allowed, scores, MASKED)
    exponent = jnp.exp(scores - jnp.max(scores, axis=-1, keepdims=True))
    weights = (exponent / jnp.sum(exponent, axis=-1, keepdims=True)).astype(jnp.bfloat16)
    attended = jnp.einsum(
        "rhst,trhd->srhd", weights, value_rows, preferred_element_type=jnp.float32
    )
    gated_rows = (attended.reshape(seq_count * res_count, inner_channel_width) * gating).astype(
        jnp.bfloat16
    )
    update = (
        jnp.dot(gated_rows, focus_exit_weights, preferred_element_type=jnp.float32)
        + focus_exit_addend
    )
    return (
        vertical_pieces.astype(jnp.float32) + update.reshape(seq_count, res_count, feature_width)
    ).astype(jnp.bfloat16)


def project_pairs(
    revised_tensor,
    present_mask,
    product_mean_layer_stretch,
    product_mean_layer_shift,
    twin_map_matrix,
    twin_map_shift,
):
    seq_count, res_count, feature_width = revised_tensor.shape
    normed = layer_norm(
        revised_tensor, product_mean_layer_stretch, product_mean_layer_shift
    ).reshape(seq_count * res_count, feature_width)
    projected = (
        jnp.dot(normed, twin_map_matrix, preferred_element_type=jnp.float32) + twin_map_shift
    )
    projected = projected.reshape(seq_count, res_count, 2 * OUTER_CHANNELS) * present_mask[
        :, :, None
    ].astype(jnp.float32)
    projected = projected.astype(jnp.bfloat16)
    return (projected[:, :, :OUTER_CHANNELS], projected[:, :, OUTER_CHANNELS:])


def pair_tile(left_rows, right_cols, live_rows, live_cols, couple_map_matrix, couple_map_shift):
    row_count = left_rows.shape[1]
    col_count = right_cols.shape[1]
    outer_sum = jnp.einsum(
        "sic,sje->ijce", left_rows, right_cols, preferred_element_type=jnp.float32
    )
    counts = jnp.einsum("si,sj->ij", live_rows, live_cols, preferred_element_type=jnp.float32)
    mean_terms = (
        outer_sum.reshape(row_count, col_count, OUTER_CHANNELS * OUTER_CHANNELS)
        / jnp.maximum(counts, 1.0)[:, :, None]
    ).astype(jnp.bfloat16)
    result = jnp.dot(
        mean_terms.reshape(row_count * col_count, OUTER_CHANNELS * OUTER_CHANNELS),
        couple_map_matrix,
        preferred_element_type=jnp.float32,
    )
    result = result + couple_map_shift
    return result.astype(jnp.bfloat16).reshape(row_count, col_count, PAIR_DIM)


def tiled_pairs(left_rows, right_cols, live_rows, live_cols, couple_map_matrix, couple_map_shift):
    return pair_tile(
        left_rows, right_cols, live_rows, live_cols, couple_map_matrix, couple_map_shift
    )


def shards(
    homolog_stack_tensor,
    occupancy_indicator,
    chain_existence_flags,
    focus_normal_factor,
    focus_normal_addend,
    probe_index_weights,
    payload_valve_weights,
    logistic_valve_addend,
    focus_exit_weights,
    focus_exit_addend,
    product_mean_layer_stretch,
    product_mean_layer_shift,
    twin_map_matrix,
    twin_map_shift,
    couple_map_matrix,
    couple_map_shift,
):
    vertical_pieces = lax.all_to_all(
        homolog_stack_tensor, "dap", split_axis=1, concat_axis=0, tiled=True
    )
    seq_count, res_local, feature_width = vertical_pieces.shape
    position = lax.axis_index("dap")
    present_integer = occupancy_indicator * chain_existence_flags[:, None]
    live_all = present_integer.astype(jnp.bfloat16)
    live_own = lax.dynamic_slice_in_dim(present_integer, position * res_local, res_local, 1)
    revised_tensor = heed_across_lanes(
        vertical_pieces,
        live_own,
        focus_normal_factor,
        focus_normal_addend,
        probe_index_weights,
        payload_valve_weights,
        logistic_valve_addend,
        focus_exit_weights,
        focus_exit_addend,
    )
    left_own, right_own = project_pairs(
        revised_tensor,
        live_own,
        product_mean_layer_stretch,
        product_mean_layer_shift,
        twin_map_matrix,
        twin_map_shift,
    )
    live_rows = live_own.astype(jnp.bfloat16)
    pair_rows = tiled_pairs(
        left_own,
        lax.all_gather(right_own, "dap", axis=1, tiled=True),
        live_rows,
        live_all,
        couple_map_matrix,
        couple_map_shift,
    )
    return (revised_tensor, pair_rows)


def solution(mesh):
    in_specs = (
        P(("grp", "dap"), None, None),
        P("grp", None),
        P("grp"),
        P(),
        P(),
        P(),
        P(),
        P(),
        P(),
        P(),
        P(),
        P(),
        P(),
        P(),
        P(),
        P(),
    )
    out_specs = (P("grp", "dap", None), P(("grp", "dap"), None, None))
    return jax.shard_map(shards, mesh=mesh, in_specs=in_specs, out_specs=out_specs, check_vma=False)
```

profile of v0, /device:TPU:0, one launch (start us, length us, event | category | flops | bytes accessed | tf_op | source)
XLA Modules:
  0.0 49.4 jit_solution(6411777289907106998)
XLA Ops:
  0.6 1.6 %copy.54 = bf16[2,64,256]{2,0,1:T(2,128)(2,1)} copy(bf16[2,64,256]{2,1,0:T(8,128)(2,1)} %param.16) | data formatting | bytes 131072 | tf_op args[0]
  2.2 7.4 %all-to-all-start = ((bf16[2,64,256]{2,0,1:T(2,128)(2,1)}), bf16[2,64,256]{2,0,1:T(2,128)(2,1)S(1)}, u32[]{:S(2)}, u32[]{:S(2)}) async-start(bf16[2,64,256]{2,0,1:T(2,128)(2,1)} %copy.54), calls=%async_computation | async-start | bytes 131072 | tf_op jit(solution)/shard_map/all_to_all | solution.py:139
  9.7 0.8 %copy.56 = s32[32,64]{0,1:T(8,128)S(1)} copy(s32[32,64]{1,0:T(8,128)} %param.17) | data formatting | bytes 16384 | tf_op args[1]
  10.4 0.7 %broadcast_multiply_fusion = s32[32,64]{0,1:T(8,128)S(1)} fusion(s32[32,64]{0,1:T(8,128)S(1)} %copy.56, s32[32]{0:T(128)} %param.18), kind=kLoop, calls=%fused_computation.50 | loop fusion | flops 2048 | bytes 16512 | tf_op jit(solution)/shard_map/mul | solution.py:144
  11.3 5.2 %all-to-all-done = bf16[2,64,256]{2,0,1:T(2,128)(2,1)S(1)} async-done(((bf16[2,64,256]{2,0,1:T(2,128)(2,1)}), bf16[2,64,256]{2,0,1:T(2,128)(2,1)S(1)}, u32[]{:S(2)}, u32[]{:S(2)}) %all-to-all-start) | async-done | bytes 65568 | tf_op jit(solution)/shard_map/all_to_all | solution.py:139
  16.8 0.2 multiply_reduce_fusion
  17.3 1.0 %fusion.38 = f32[128,512]{1,0:T(8,128)S(1)} fusion(bf16[256,512]{1,0:T(8,128)(2,1)S(1)} %copy-done, f32[128,256]{1,0:T(8,128)S(1)} %reshape.129, f32[256]{0:T(256)} %param.20, f32[256]{0:T(256)} %param.19, f32[128]{0:T(128)S(1)} %rsqrt.20, f32[128]{0:T(128)S(1)} %div.37), kind=kOutput, calls=%fused_computation.63 | convolution fusion | flops 33718272 | bytes 658432 | tf_op jit(solution)/shard_map/dot_general | solution.py:40
  18.7 0.3 fusion.40
  19.1 0.3 convolution_select_fusion
  19.4 0.2 fusion.39
  19.9 0.3 convolution_bitcast_fusion.1
  20.3 0.5 copy.61
  20.7 0.2 reshape.123
  20.9 0.3 convert_reduce_fusion
  21.2 0.2 fusion.10
  21.5 0.2 convolution_add_fusion.2
  22.0 0.7 %reshape.124 = f32[32,4,256]{2,1,0:T(4,128)} reshape(f32[128,256]{1,0:T(8,128)S(1)} %get-tuple-element.4) | data formatting | bytes 262144 | tf_op jit(solution)/shard_map/reshape | solution.py:69
  22.7 19.1 %all_gather.3 = bf16[32,64,32]{2,0,1:T(8,128)(2,1)S(1)} all-gather(bf16[32,4,32]{2,0,1:T(8,128)(2,1)S(1)} %copy.64), channel_id=1, replica_groups=mesh['grp'=2,'dap'=16] {'dap'}, dimensions={1}, use_global_device_ids=true | all-gather | bytes 139264 | tf_op jit(solution)/shard_map/all_gather | solution.py:169
  41.9 0.9 %copy.68 = bf16[32,64,32,1]{0,1,3,2:T(8,128)(2,1)S(1)} copy(bf16[32,64,32,1]{2,0,1,3:T(8,128)(2,1)S(1)} %bitcast.36) | data formatting | bytes 262144 | tf_op jit(solution)/shard_map/all_gather | solution.py:169
  42.7 0.7 %convolution_bitcast_fusion = f32[4,64,32,32]{1,2,0,3:T(8,128)S(1)} fusion(bf16[32,64,32,1]{0,1,3,2:T(8,128)(2,1)S(1)} %copy.68, bf16[32,4,64]{0,2,1:T(8,128)(2,1)S(1)} %multiply_convert_fusion), kind=kOutput, calls=%fused_computation.1 | convolution fusion | flops 16777216 | bytes 1605632 | tf_op jit(solution)/shard_map/sic,sje->ijce/dot_general | solution.py:98
  43.4 1.4 %copy.66 = f32[4,64,32,32]{1,0,3,2:T(4,128)S(1)} copy(f32[4,64,32,32]{1,2,0,3:T(8,128)S(1)} %convolution_bitcast_fusion) | data formatting | bytes 2097152 | tf_op jit(solution)/shard_map/sic,sje->ijce/transpose | solution.py:98
  44.8 1.1 %reshape.126 = f32[256,1024]{0,1:T(8,128)S(1)} reshape(f32[4,64,32,32]{1,0,3,2:T(4,128)S(1)} %copy.66) | data formatting | bytes 2097152 | tf_op jit(solution)/shard_map/reshape | solution.py:103
  45.9 1.6 %fusion.20 = bf16[32,4,256]{2,1,0:T(4,128)(2,1)} fusion(f32[32,4,256]{2,1,0:T(4,128)} %reshape.124, f32[2,16,4,256]{3,2,0,1:T(4,128)S(1)} %copy.55), kind=kLoop, calls=%fused_computation.36 | loop fusion | flops 65536 | bytes 327680 | tf_op jit(solution)/shard_map/convert_element_type | solution.py:70
  47.5 1.9 %fusion.3 = bf16[256,128]{1,0:T(8,128)(2,1)} fusion(bf16[1024,128]{1,0:T(8,128)(2,1)} %param.30, f32[256,1024]{0,1:T(8,128)S(1)} %reshape.126, f32[256]{0:T(256)S(1)} %div.44, f32[128]{0:T(128)S(1)} %copy-done.11), kind=kOutput, calls=%fused_computation.8 | convolution fusion | flops 67698688 | bytes 1377792 | tf_op jit(solution)/shard_map/dot_general | solution.py:106
  (50 shorter events, 1.7 us)
Async XLA Ops:
  0.6 16.7 %copy-start = (bf16[256,512]{1,0:T(8,128)(2,1)S(1)}, bf16[256,512]{1,0:T(8,128)(2,1)}, u32[]{:S(2)}) copy-start(bf16[256,512]{1,0:T(8,128)(2,1)} %param.21) | copy-start | bytes 786436
  2.2 14.3 %all-to-all-start = ((bf16[2,64,256]{2,0,1:T(2,128)(2,1)}), bf16[2,64,256]{2,0,1:T(2,128)(2,1)S(1)}, u32[]{:S(2)}, u32[]{:S(2)}) async-start(bf16[2,64,256]{2,0,1:T(2,128)(2,1)} %copy.54), calls=%async_computation | async-start | bytes 131072 | tf_op jit(solution)/shard_map/all_to_all | solution.py:139
  17.3 2.1 %copy-start.1 = (bf16[256,512]{1,0:T(8,128)(2,1)S(1)}, bf16[256,512]{1,0:T(8,128)(2,1)}, u32[]{:S(2)}) copy-start(bf16[256,512]{1,0:T(8,128)(2,1)} %param.22) | copy-start | bytes 786436
  17.3 2.1 %copy-start.2 = (f32[256]{0:T(256)S(1)}, f32[256]{0:T(256)}, u32[]{:S(2)}) copy-start(f32[256]{0:T(256)} %param.20) | copy-start | bytes 3076
  17.3 2.1 %copy-start.3 = (f32[256]{0:T(256)S(1)}, f32[256]{0:T(256)}, u32[]{:S(2)}) copy-start(f32[256]{0:T(256)} %param.19) | copy-start | bytes 3076
  19.8 1.1 %copy-start.4 = (bf16[256,256]{1,0:T(8,128)(2,1)S(1)}, bf16[256,256]{1,0:T(8,128)(2,1)}, u32[]{:S(2)}) copy-start(bf16[256,256]{1,0:T(8,128)(2,1)} %param.24) | copy-start | bytes 393220
  19.8 1.1 %copy-start.6 = (f32[256]{0:T(256)S(1)}, f32[256]{0:T(256)}, u32[]{:S(2)}) copy-start(f32[256]{0:T(256)} %param.25) | copy-start | bytes 3076
  19.8 1.1 %copy-start.7 = (f32[256]{0:T(256)S(1)}, f32[256]{0:T(256)}, u32[]{:S(2)}) copy-start(f32[256]{0:T(256)} %param.23) | copy-start | bytes 3076
  19.9 1.6 %copy-start.5 = (bf16[256,64]{0,1:T(8,128)(2,1)S(1)}, bf16[256,64]{0,1:T(8,128)(2,1)}, u32[]{:S(2)}) copy-start(bf16[256,64]{0,1:T(8,128)(2,1)} %param.28) | copy-start | bytes 98308
  19.9 1.6 %copy-start.8 = (f32[256]{0:T(256)S(1)}, f32[256]{0:T(256)}, u32[]{:S(2)}) copy-start(f32[256]{0:T(256)} %param.27) | copy-start | bytes 3076
  19.9 1.6 %copy-start.9 = (f32[256]{0:T(256)S(1)}, f32[256]{0:T(256)}, u32[]{:S(2)}) copy-start(f32[256]{0:T(256)} %param.26) | copy-start | bytes 3076
  19.9 1.6 %copy-start.10 = (f32[64]{0:T(128)S(1)}, f32[64]{0:T(128)}, u32[]{:S(2)}) copy-start(f32[64]{0:T(128)} %param.29) | copy-start | bytes 772
  44.8 2.7 %copy-start.11 = (f32[128]{0:T(128)S(1)}, f32[128]{0:T(128)}, u32[]{:S(2)}) copy-start(f32[128]{0:T(128)} %param.31) | copy-start | bytes 1540
where the time goes:
time: 49.8 us; the launch traced here: 49.4 us
  blocking collectives  19.1 us (38%)
  local copies, waits for them, and re-layouts  8.33 us (17%)
  starting transfers between devices  7.41 us (15%)
  matrix products  5.4 us (11%)
  waiting for transfers between devices  5.2 us (10%)
  other arithmetic  2.89 us (6%)
  between operations  1.03 us (2%)
    all_gather x1, blocking collectives, shards(): lax.all_gather(right_own, 'dap', axis=1, tiled=True)  19.1 us
    all_to_all x1, starting transfers between devices, shards(): lax.all_to_all(homolog_stack_tensor, 'dap', split_axis=1, concat_axis=0,...  7.41 us
    all_to_all x1, waiting for transfers between devices, shards(): lax.all_to_all(homolog_stack_tensor, 'dap', split_axis=1, concat_axis=0,...  5.2 us
    unnamed x26, local copies, waits for them, and re-layouts  2.46 us
    dot_general x1, matrix products, pair_tile(): jnp.dot(mean_terms.reshape(row_count * col_count, OUTER_CHANNELS * OUTER_...  1.93 us
    convert_element_type x1, other arithmetic, heed_across_lanes(): return (vertical_pieces.astype(jnp.float32) + update.reshape(seq_count, r...  1.58 us
    transpose x1, local copies, waits for them, and re-layouts, pair_tile(): jnp.einsum('sic,sje->ijce', left_rows, right_cols, preferred_element_type...  1.35 us
    reshape x1, local copies, waits for them, and re-layouts, pair_tile(): outer_sum.reshape(row_count, col_count, OUTER_CHANNELS * OUTER_CHANNELS)  1.13 us
  transfers between devices with their start and end apart: 1, of which 1 were waited for; matrix products, arithmetic and copies ran while one was open for 3% of the time, Pallas kernels for 0%

commit v1 on v0

--- a/solution.py
+++ b/solution.py
@@ -1,6 +1,9 @@
 import jax
 import jax.numpy as jnp
+import numpy as np
 from jax import lax
+from jax.experimental import pallas as pl
+from jax.experimental.pallas import tpu as pltpu
 from jax.sharding import PartitionSpec as P
 
 HEAD_COUNT = 8
@@ -175,7 +178,247 @@
     return (revised_tensor, pair_rows)
 
 
+FUSED_ROWS = 128
+
+
+def normalise(rows, scale_row, shift_row):
+    centred = rows - jnp.mean(rows, axis=-1, keepdims=True)
+    variance = jnp.mean(centred * centred, axis=-1, keepdims=True)
+    return (centred * lax.rsqrt(variance + EPSILON) * scale_row + shift_row).astype(jnp.bfloat16)
+
+
+def column_kernel(
+    x_ref,
+    order_ref,
+    live_ref,
+    factor_ref,
+    addend_ref,
+    probe_ref,
+    valve_ref,
+    valve_addend_ref,
+    exit_ref,
+    exit_addend_ref,
+    stretch_ref,
+    shift_ref,
+    twin_ref,
+    twin_shift_ref,
+    expand_ref,
+    sum_ref,
+    revised_ref,
+    left_ref,
+    right_ref,
+    *,
+    seq_count,
+):
+    rows, width = x_ref.shape
+    inner = HEAD_COUNT * HEAD_CHANNELS
+    f32 = jnp.float32
+    bf16 = jnp.bfloat16
+    x = jnp.dot(order_ref[...], x_ref[...], preferred_element_type=f32)
+    normed = normalise(x, factor_ref[...], addend_ref[...])
+    query_key = jnp.dot(normed, probe_ref[...], preferred_element_type=f32)
+    value_gate = jnp.dot(normed, valve_ref[...], preferred_element_type=f32)
+    query = (query_key[:, :inner] * HEAD_CHANNELS ** (-0.5)).astype(bf16)
+    key = query_key[:, inner:].astype(bf16)
+    value = value_gate[:, :inner].astype(bf16)
+    gating = jax.nn.sigmoid(value_gate[:, inner:] + valve_addend_ref[...])
+    lane = lax.broadcasted_iota(jnp.int32, (rows, inner), 1)
+    zero = jnp.zeros((rows, inner), bf16)
+    heads = [
+        (lane >= h * HEAD_CHANNELS) & (lane < (h + 1) * HEAD_CHANNELS) for h in range(HEAD_COUNT)
+    ]
+    query_heads = jnp.concatenate([jnp.where(m, query, zero) for m in heads], axis=0)
+    value_heads = jnp.concatenate([jnp.where(m, value, zero) for m in heads], axis=0)
+    scores = lax.dot_general(
+        query_heads, key, (((1,), (1,)), ((), ())), preferred_element_type=f32
+    ).reshape(HEAD_COUNT, rows, rows)
+    row_at = lax.broadcasted_iota(jnp.int32, (rows, rows), 0)
+    col_at = lax.broadcasted_iota(jnp.int32, (rows, rows), 1)
+    same = None
+    for r in range(rows // seq_count):
+        low, high = r * seq_count, (r + 1) * seq_count
+        block = (row_at >= low) & (row_at < high) & (col_at >= low) & (col_at < high)
+        same = block if same is None else same | block
+    live = jnp.broadcast_to(live_ref[...], (rows, rows))
+    allowed = same & (live > 0.0)
+    other = jnp.where(same, MASKED, -jnp.inf)
+    scores = jnp.where(allowed[None], scores, other[None])
+    exponent = jnp.exp(scores - jnp.max(scores, axis=-1, keepdims=True))
+    weights = (exponent / jnp.sum(exponent, axis=-1, keepdims=True)).astype(bf16)
+    weights = jnp.concatenate([weights[h] for h in range(HEAD_COUNT)], axis=1)
+    attended = jnp.dot(weights, value_heads, preferred_element_type=f32)
+    gated = (attended * gating).astype(bf16)
+    update = jnp.dot(gated, exit_ref[...], preferred_element_type=f32) + exit_addend_ref[...]
+    revised = (x + update).astype(bf16)
+    revised_ref[...] = revised
+    normed = normalise(revised.astype(f32), stretch_ref[...], shift_ref[...])
+    projected = lax.dot_general(
+        normed, twin_ref[...], (((1,), (1,)), ((), ())), preferred_element_type=f32
+    )
+    live_col = jnp.sum(jnp.where(row_at == col_at, live, 0.0), axis=1, keepdims=True)
+    projected = ((projected + twin_shift_ref[...]) * live_col).astype(bf16)
+    left_ref[...] = projected[:, :OUTER_CHANNELS]
+    spread = jnp.dot(projected, expand_ref[...], preferred_element_type=f32)
+    wide = spread.shape[1]
+    seq_row = lax.broadcasted_iota(jnp.int32, (rows, wide), 0) & (seq_count - 1)
+    seq_col = lax.broadcasted_iota(jnp.int32, (rows, wide), 1) & (seq_count - 1)
+    spread = jnp.where(seq_row == seq_col, spread, 0.0).astype(bf16)
+    packed = jnp.dot(sum_ref[...], spread, preferred_element_type=f32)
+    right_ref[...] = packed[: right_ref.shape[0]].astype(bf16)
+
+
+def left_kernel(left_ref, couple_ref, out_ref, *, seq_count):
+    rows = left_ref.shape[0]
+    left = left_ref[...]
+    for e in range(OUTER_CHANNELS):
+        lanes = slice(e * PAIR_DIM, (e + 1) * PAIR_DIM)
+        term = jnp.dot(left, couple_ref[:, lanes], preferred_element_type=jnp.float32)
+        term = term.astype(jnp.bfloat16)
+        for i in range(rows // seq_count):
+            out_ref[e * seq_count : (e + 1) * seq_count, i * PAIR_DIM : (i + 1) * PAIR_DIM] = term[
+                i * seq_count : (i + 1) * seq_count
+            ]
+
+
+def pair_kernel(right_ref, terms_ref, scale_ref, shift_ref, out_ref):
+    result = jnp.dot(right_ref[...], terms_ref[...], preferred_element_type=jnp.float32)
+    for i in range(out_ref.shape[0]):
+        own = result[:, i * PAIR_DIM : (i + 1) * PAIR_DIM] * scale_ref[:, i : i + 1]
+        out_ref[i] = (own + shift_ref[...]).astype(jnp.bfloat16)
+
+
+def collect(block, axis_size, position):
+    if axis_size & (axis_size - 1):
+        return lax.all_gather(block, "dap", axis=0, tiled=True)
+    step = 1
+    while step < axis_size:
+        pairs = [(j, j ^ step) for j in range(axis_size)]
+        other = lax.ppermute(block, "dap", pairs)
+        upper = (position & step) > 0
+        block = jnp.where(
+            upper,
+            jnp.concatenate([other, block], axis=0),
+            jnp.concatenate([block, other], axis=0),
+        )
+        step *= 2
+    return block
+
+
+def fused_shards(
+    homolog_stack_tensor,
+    occupancy_indicator,
+    chain_existence_flags,
+    focus_normal_factor,
+    focus_normal_addend,
+    probe_index_weights,
+    payload_valve_weights,
+    logistic_valve_addend,
+    focus_exit_weights,
+    focus_exit_addend,
+    product_mean_layer_stretch,
+    product_mean_layer_shift,
+    twin_map_matrix,
+    twin_map_shift,
+    couple_map_matrix,
+    couple_map_shift,
+    axis_size,
+):
+    seq_local, res_count, width = homolog_stack_tensor.shape
+    res_local = res_count // axis_size
+    seq_count = seq_local * axis_size
+    rows = seq_count * res_local
+    bf16 = jnp.bfloat16
+    sent = homolog_stack_tensor.reshape(seq_local, axis_size, res_local, width)
+    sent = jnp.transpose(sent, (1, 2, 0, 3)).reshape(axis_size, res_local * seq_local, width)
+    got = lax.all_to_all(sent, "dap", split_axis=0, concat_axis=0, tiled=True)
+    got = got.reshape(rows, width)
+    position = lax.axis_index("dap")
+    present = occupancy_indicator * chain_existence_flags[:, None]
+    live_own = lax.dynamic_slice_in_dim(present, position * res_local, res_local, 1)
+    live_row = jnp.transpose(live_own).reshape(1, rows).astype(jnp.float32)
+    counts = jnp.einsum(
+        "sj,si->ji",
+        present.astype(bf16),
+        live_own.astype(bf16),
+        preferred_element_type=jnp.float32,
+    )
+    scale = 1.0 / jnp.maximum(counts, 1.0)
+    at = np.arange(rows)
+    res_at, seq_at = at // seq_count, at % seq_count
+    source = (seq_at // seq_local) * res_local * seq_local + res_at * seq_local + seq_at % seq_local
+    order = jnp.asarray(source[:, None] == at[None, :], bf16)
+    wide = OUTER_CHANNELS * seq_count
+    expand = jnp.asarray(
+        np.arange(2 * OUTER_CHANNELS)[:, None] == OUTER_CHANNELS + np.arange(wide)[None, :] // seq_count,
+        bf16,
+    )
+    res_pad = -(-res_local // 8) * 8
+    summing = jnp.asarray(np.arange(res_pad)[:, None] == res_at[None, :], bf16)
+    as_row = lambda v: v.reshape(1, -1)
+    vmem = pl.BlockSpec(memory_space=pltpu.VMEM)
+    revised, left, right = pl.pallas_call(
+        lambda *refs: column_kernel(*refs, seq_count=seq_count),
+        out_shape=(
+            jax.ShapeDtypeStruct((rows, width), bf16),
+            jax.ShapeDtypeStruct((rows, OUTER_CHANNELS), bf16),
+            jax.ShapeDtypeStruct((res_local, wide), bf16),
+        ),
+        in_specs=[vmem] * 16,
+        out_specs=(vmem, vmem, vmem),
+        name="column",
+    )(
+        got,
+        order,
+        live_row,
+        as_row(focus_normal_factor),
+        as_row(focus_normal_addend),
+        probe_index_weights,
+        payload_valve_weights,
+        as_row(logistic_valve_addend),
+        focus_exit_weights,
+        as_row(focus_exit_addend),
+        as_row(product_mean_layer_stretch),
+        as_row(product_mean_layer_shift),
+        jnp.transpose(twin_map_matrix),
+        as_row(twin_map_shift),
+        expand,
+        summing,
+    )
+    terms = pl.pallas_call(
+        lambda *refs: left_kernel(*refs, seq_count=seq_count),
+        out_shape=jax.ShapeDtypeStruct((wide, res_local * PAIR_DIM), bf16),
+        in_specs=[vmem] * 2,
+        out_specs=vmem,
+        cost_estimate=pl.CostEstimate(
+            flops=4 * rows * OUTER_CHANNELS * OUTER_CHANNELS * PAIR_DIM,
+            bytes_accessed=2 * wide * res_local * PAIR_DIM,
+            transcendentals=0,
+        ),
+        name="terms",
+    )(left, couple_map_matrix.reshape(OUTER_CHANNELS, OUTER_CHANNELS * PAIR_DIM))
+    alignment_after = jnp.transpose(revised.reshape(res_local, seq_count, width), (1, 0, 2))
+    right_all = collect(right, axis_size, position)
+    pair_rows = pl.pallas_call(
+        pair_kernel,
+        out_shape=jax.ShapeDtypeStruct((res_local, res_count, PAIR_DIM), bf16),
+        in_specs=[vmem] * 4,
+        out_specs=vmem,
+        name="pairs",
+    )(right_all, terms, scale, as_row(couple_map_shift))
+    return (alignment_after, pair_rows)
+
+
 def solution(mesh):
+    axis_size = mesh.shape["dap"]
+
+    def step(*arrays):
+        seq_local, res_count, _ = arrays[0].shape
+        seq_count = seq_local * axis_size
+        rows = seq_count * (res_count // axis_size)
+        if rows <= FUSED_ROWS and seq_count & (seq_count - 1) == 0 and seq_count % 16 == 0:
+            return fused_shards(*arrays, axis_size)
+        return shards(*arrays)
+
     in_specs = (
         P(("grp", "dap"), None, None),
         P("grp", None),
@@ -195,4 +438,4 @@
         P(),
     )
     out_specs = (P("grp", "dap", None), P(("grp", "dap"), None, None))
-    return jax.shard_map(shards, mesh=mesh, in_specs=in_specs, out_specs=out_specs, check_vma=False)
+    return jax.shard_map(step, mesh=mesh, in_specs=in_specs, out_specs=out_specs, check_vma=False)

time: 49.8 us -> 39.8 us (0.80)
  blocking collectives: 19.1 us -> 0 us
  waiting for transfers between devices: 5.2 us -> 15.3 us
  Pallas kernels: 0 us -> 8.24 us
  matrix products: 5.4 us -> 0.81 us
  local copies, waits for them, and re-layouts: 8.33 us -> 4.46 us
  other arithmetic: 2.89 us -> 1.62 us
  starting transfers between devices: 7.41 us -> 8.2 us
    all_gather x1 -> x0, blocking collectives: 19.1 us -> none  [shards(): lax.all_gather(right_own, 'dap', axis=1, tiled=True)]
    ppermute x0 -> x4, waiting for transfers between devices: none -> 9.32 us  [collect(): other = lax.ppermute(block, 'dap', pairs)]
    pallas_call x0 -> x3, Pallas kernels: none -> 8.24 us  [the longest x1 3.74 us: fused_shards(): pl.pallas_call(lambda *refs: column_kernel(*refs, seq_count=seq_count), o...]
    dot_general x9 -> x1, matrix products: 5.06 us -> 0.81 us  [fused_shards(): jnp.einsum('sj,si->ji', present.astype(bf16), live_own.astype(bf16), pref...]
    unnamed x26 -> x10, local copies, waits for them, and re-layouts: 2.46 us -> 0.66 us
    transpose x2 -> x1, local copies, waits for them, and re-layouts: 1.81 us -> 0.07 us  [fused_shards(): jnp.transpose(sent, (1, 2, 0, 3))]
    convert_element_type x5 -> x1, other arithmetic: 1.66 us -> 0.08 us  [fused_shards(): live_row = jnp.transpose(live_own).reshape(1, rows).astype(jnp.float32)]
    select_n x0 -> x4, other arithmetic: none -> 1.48 us  [collect(): jnp.where(upper, jnp.concatenate([other, block], axis=0), jnp.concatenate...]
  transfers between devices with their start and end apart: 1 -> 5, of which waited for: 1 -> 5; matrix products, arithmetic and copies ran while one was open for 3% -> 8% of each run, Pallas kernels for 0% -> 6%
where the time goes in v1:
time: 39.8 us; the launch traced here: 39.4 us
  waiting for transfers between devices  15.3 us (38%)
  Pallas kernels  8.24 us (21%)
  starting transfers between devices  8.2 us (21%)
  local copies, waits for them, and re-layouts  4.46 us (11%)
  other arithmetic  1.62 us (4%)
  matrix products  0.81 us (2%)
  between operations  0.69 us (2%)
    ppermute x4, waiting for transfers between devices, collect(): other = lax.ppermute(block, 'dap', pairs)  9.32 us
    all_to_all x1, starting transfers between devices, fused_shards(): got = lax.all_to_all(sent, 'dap', split_axis=0, concat_axis=0, tiled=True)  7.55 us
    all_to_all x1, waiting for transfers between devices, fused_shards(): got = lax.all_to_all(sent, 'dap', split_axis=0, concat_axis=0, tiled=True)  6.02 us
    pallas_call x1, Pallas kernels, fused_shards(): pl.pallas_call(lambda *refs: column_kernel(*refs, seq_count=seq_count), o...  3.74 us
    pallas_call x1, Pallas kernels, fused_shards(): pl.pallas_call(lambda *refs: left_kernel(*refs, seq_count=seq_count), out...  2.34 us
    pallas_call x1, Pallas kernels, fused_shards(): pl.pallas_call(pair_kernel, out_shape=jax.ShapeDtypeStruct((res_local, re...  2.16 us
    select_n x4, other arithmetic, collect(): jnp.where(upper, jnp.concatenate([other, block], axis=0), jnp.concatenate...  1.48 us
    reshape x1, local copies, waits for them, and re-layouts, fused_shards(): sent = homolog_stack_tensor.reshape(seq_local, axis_size, res_local, width)  0.86 us
  transfers between devices with their start and end apart: 5, of which 5 were waited for; matrix products, arithmetic and copies ran while one was open for 8% of the time, Pallas kernels for 6%

profile of v1, /device:TPU:0, one launch (start us, length us, event | category | flops | bytes accessed | tf_op | source)
XLA Modules:
  0.0 39.4 jit_solution(9619686724910784463)
XLA Ops:
  0.6 0.9 %reshape.58 = bf16[2,16,4,256]{3,2,1,0:T(4,128)(2,1)S(1)} reshape(bf16[2,64,256]{2,1,0:T(8,128)(2,1)} %param.19) | data formatting | bytes 131072 | tf_op jit(solution)/shard_map/reshape | solution.py:331
  1.6 0.7 %reshape.59 = bf16[16,8,256]{2,1,0:T(8,128)(2,1)} reshape(bf16[16,4,2,256]{3,2,1,0:T(2,128)(2,1)S(1)} %copy.25) | data formatting | bytes 131072 | tf_op jit(solution)/shard_map/reshape | solution.py:332
  2.2 7.5 %all-to-all-start = ((bf16[16,8,256]{2,1,0:T(8,128)(2,1)}), bf16[16,8,256]{2,1,0:T(8,128)(2,1)S(1)}, u32[]{:S(2)}, u32[]{:S(2)}) async-start(bf16[16,8,256]{2,1,0:T(8,128)(2,1)} %reshape.59), calls=%async_computation | async-start | bytes 131072 | tf_op jit(solution)/shard_map/all_to_all | solution.py:333
  9.8 0.1 broadcast_multiply_fusion
  9.9 0.1 convert_bitcast_fusion
  10.0 0.1 copy.26
  10.0 0.6 %convert_element_type.15.refs_2_ = f32[1,128]{1,0:T(1,128)} reshape(f32[4,32]{1,0:T(4,128)S(1)} %copy.26) | data formatting | bytes 1024 | tf_op jit(solution)/shard_map/convert_element_type | solution.py:338
  10.7 6.0 %all-to-all-done = bf16[16,8,256]{2,1,0:T(8,128)(2,1)S(1)} async-done(((bf16[16,8,256]{2,1,0:T(8,128)(2,1)}), bf16[16,8,256]{2,1,0:T(8,128)(2,1)S(1)}, u32[]{:S(2)}, u32[]{:S(2)}) %all-to-all-start) | async-done | bytes 65568 | tf_op jit(solution)/shard_map/all_to_all | solution.py:333
  16.7 0.6 %copy-done = bf16[16,8,256]{2,1,0:T(8,128)(2,1)} copy-done((bf16[16,8,256]{2,1,0:T(8,128)(2,1)}, bf16[16,8,256]{2,1,0:T(8,128)(2,1)S(1)}, u32[]{:S(2)}) %copy-start) | copy-done | bytes 65560
  17.3 3.7 %column.1 = (bf16[128,256]{1,0:T(8,128)(2,1)}, bf16[128,32]{1,0:T(8,128)(2,1)}, bf16[4,1024]{1,0:T(4,128)(2,1)}) custom-call(bf16[128,256]{1,0:T(8,128)(2,1)} %bitcast.17, bf16[128,128]{1,0:T(8,128)(2,1)} %constant.24.clone.refs_1_, f32[1,128]{1,0:T(1,128)} %convert_element_type.15.refs_2_, f32[1,256]{1,0:T(1,128)} %bitcast.22, f32[1,256]{1,0:T(1,128)} %bitcast.23, ...), custom_call_target="tpu_custom_call" | custom-call | tf_op jit(solution)/shard_map/column/pallas_call | solution.py:359
  21.1 1.4 %collective-permute-done = bf16[4,1024]{1,0:T(4,128)(2,1)S(1)} collective-permute-done((bf16[4,1024]{1,0:T(4,128)(2,1)}, bf16[4,1024]{1,0:T(4,128)(2,1)S(1)}, u32[]{:S(2)}, u32[]{:S(2)}) %collective-permute-start) | collective-permute-done | bytes 8224 | tf_op jit(solution)/shard_map/ppermute | solution.py:296
  22.4 0.8 %maximum_select_fusion.3 = bf16[8,1024]{1,0:T(8,128)(2,1)S(1)} fusion(bf16[4,1024]{1,0:T(4,128)(2,1)} %get-tuple-element.6, bf16[4,1024]{1,0:T(4,128)(2,1)S(1)} %collective-permute-done, pred[]{:T(512)S(6)} %gt.15), kind=kLoop, calls=%fused_computation.6 | loop fusion | flops 73728 | bytes 32769 | tf_op jit(solution)/shard_map/jit(_where)/select_n | solution.py:298
  23.2 0.2 collective-permute-start.1
  23.4 3.6 %collective-permute-done.1 = bf16[8,1024]{1,0:T(8,128)(2,1)S(1)} collective-permute-done((bf16[8,1024]{1,0:T(8,128)(2,1)S(1)}, bf16[8,1024]{1,0:T(8,128)(2,1)S(1)}, u32[]{:S(2)}, u32[]{:S(2)}) %collective-permute-start.1) | collective-permute-done | bytes 16416 | tf_op jit(solution)/shard_map/ppermute | solution.py:296
  27.1 0.2 collective-permute-start.2
  27.2 3.8 %collective-permute-done.2 = bf16[16,1024]{1,0:T(8,128)(2,1)S(1)} collective-permute-done((bf16[16,1024]{1,0:T(8,128)(2,1)S(1)}, bf16[16,1024]{1,0:T(8,128)(2,1)S(1)}, u32[]{:S(2)}, u32[]{:S(2)}) %collective-permute-start.2) | collective-permute-done | bytes 32800 | tf_op jit(solution)/shard_map/ppermute | solution.py:296
  31.0 0.3 collective-permute-start.3
  31.3 0.8 %fusion.scale_ref = f32[64,4]{1,0:T(8,128)} fusion(s32[32,64]{1,0:T(8,128)S(1)} %broadcast_multiply_fusion, s32[]{:T(128)S(6)} %select_n.35), kind=kOutput, calls=%fused_computation.1 | convolution fusion | flops 19072 | bytes 33796 | tf_op jit(solution)/shard_map/sj,si->ji/dot_general | solution.py:339
  32.1 0.8 %reshape.69.refs_1_ = bf16[32,4096]{1,0:T(8,128)(2,1)} reshape(bf16[1024,128]{1,0:T(8,128)(2,1)S(1)} %copy-done.1) | data formatting | bytes 524288 | tf_op jit(solution)/shard_map/reshape | solution.py:398
  33.0 0.7 %copy.33 = bf16[4,32,256]{2,0,1:T(4,128)(2,1)} copy(bf16[4,32,256]{2,1,0:T(8,128)(2,1)S(1)} %bitcast.19) | data formatting | bytes 131072 | tf_op jit(solution)/shard_map/reshape | solution.py:399
  33.7 2.3 %terms.1.terms_ref = bf16[1024,512]{1,0:T(8,128)(2,1)} custom-call(bf16[128,32]{1,0:T(8,128)(2,1)} %get-tuple-element.7.refs_0_, bf16[32,4096]{1,0:T(8,128)(2,1)} %reshape.69.refs_1_), custom_call_target="tpu_custom_call" | custom-call | flops 67108864 | bytes 1048576 | tf_op jit(solution)/shard_map/terms/pallas_call | solution.py:387
  36.0 0.5 %collective-permute-done.3 = bf16[32,1024]{1,0:T(8,128)(2,1)S(1)} collective-permute-done((bf16[32,1024]{1,0:T(8,128)(2,1)S(1)}, bf16[32,1024]{1,0:T(8,128)(2,1)S(1)}, u32[]{:S(2)}, u32[]{:S(2)}) %collective-permute-start.3) | collective-permute-done | bytes 65568 | tf_op jit(solution)/shard_map/ppermute | solution.py:296
  36.5 0.7 %maximum_select_fusion.right_ref = bf16[64,1024]{1,0:T(8,128)(2,1)} fusion(bf16[32,1024]{1,0:T(8,128)(2,1)S(1)} %maximum_select_fusion.1, bf16[32,1024]{1,0:T(8,128)(2,1)S(1)} %collective-permute-done.3, pred[]{:T(512)S(6)} %gt.12), kind=kLoop, calls=%fused_computation.2 | loop fusion | flops 589824 | bytes 262145 | tf_op jit(solution)/shard_map/jit(_where)/select_n | solution.py:298
  37.2 2.2 %pairs.1 = bf16[4,64,128]{2,1,0:T(8,128)(2,1)} custom-call(bf16[64,1024]{1,0:T(8,128)(2,1)} %maximum_select_fusion.right_ref, bf16[1024,512]{1,0:T(8,128)(2,1)} %terms.1.terms_ref, f32[64,4]{1,0:T(8,128)} %fusion.scale_ref, f32[1,128]{1,0:T(1,128)} %bitcast.29), custom_call_target="tpu_custom_call" | custom-call | tf_op jit(solution)/shard_map/pairs/pallas_call | solution.py:401
  (13 shorter events, 0.1 us)
Async XLA Ops:
  2.2 7.6 %copy-start.3 = (s32[32,64]{1,0:T(8,128)S(1)}, s32[32,64]{1,0:T(8,128)}, u32[]{:S(2)}) copy-start(s32[32,64]{1,0:T(8,128)} %param.20) | copy-start | bytes 24580
  2.2 7.6 %copy-start.4 = (s32[32]{0:T(128)S(1)}, s32[32]{0:T(128)}, u32[]{:S(2)}) copy-start(s32[32]{0:T(128)} %param.21) | copy-start | bytes 388
  2.2 14.4 %all-to-all-start = ((bf16[16,8,256]{2,1,0:T(8,128)(2,1)}), bf16[16,8,256]{2,1,0:T(8,128)(2,1)S(1)}, u32[]{:S(2)}, u32[]{:S(2)}) async-start(bf16[16,8,256]{2,1,0:T(8,128)(2,1)} %reshape.59), calls=%async_computation | async-start | bytes 131072 | tf_op jit(solution)/shard_map/all_to_all | solution.py:333
  16.7 0.6 %copy-start = (bf16[16,8,256]{2,1,0:T(8,128)(2,1)}, bf16[16,8,256]{2,1,0:T(8,128)(2,1)S(1)}, u32[]{:S(2)}) copy-start(bf16[16,8,256]{2,1,0:T(8,128)(2,1)S(1)} %all-to-all-done) | copy-start | bytes 196612
  21.1 11.1 %copy-start.1 = (bf16[1024,128]{1,0:T(8,128)(2,1)S(1)}, bf16[1024,128]{1,0:T(8,128)(2,1)}, u32[]{:S(2)}) copy-start(bf16[1024,128]{1,0:T(8,128)(2,1)} %param.33) | copy-start | bytes 786436
  21.1 1.4 %collective-permute-start = (bf16[4,1024]{1,0:T(4,128)(2,1)}, bf16[4,1024]{1,0:T(4,128)(2,1)S(1)}, u32[]{:S(2)}, u32[]{:S(2)}) collective-permute-start(bf16[4,1024]{1,0:T(4,128)(2,1)} %get-tuple-element.6), channel_id=1, source_target_pairs={{0,1},{1,0},{2,3},{3,2},{4,5},{5,4},{6,7},{7,6},{8,9},{9,8},{10,11... | collective-permute-start | bytes 24584 | tf_op jit(solution)/shard_map/ppermute | solution.py:296
  23.2 3.8 %collective-permute-start.1 = (bf16[8,1024]{1,0:T(8,128)(2,1)S(1)}, bf16[8,1024]{1,0:T(8,128)(2,1)S(1)}, u32[]{:S(2)}, u32[]{:S(2)}) collective-permute-start(bf16[8,1024]{1,0:T(8,128)(2,1)S(1)} %maximum_select_fusion.3), channel_id=1, source_target_pairs={{0,2},{1,3},{2,0},{3,1},{4,6},{5,7},{6,4},{7,5},{8,10},{9,11},{10,... | collective-permute-start | bytes 49160 | tf_op jit(solution)/shard_map/ppermute | solution.py:296
  27.1 4.0 %collective-permute-start.2 = (bf16[16,1024]{1,0:T(8,128)(2,1)S(1)}, bf16[16,1024]{1,0:T(8,128)(2,1)S(1)}, u32[]{:S(2)}, u32[]{:S(2)}) collective-permute-start(bf16[16,1024]{1,0:T(8,128)(2,1)S(1)} %maximum_select_fusion.2), channel_id=1, source_target_pairs={{0,4},{1,5},{2,6},{3,7},{4,0},{5,1},{6,2},{7,3},{8,12},{9,13},{10,... | collective-permute-start | bytes 98312 | tf_op jit(solution)/shard_map/ppermute | solution.py:296
  31.0 5.5 %collective-permute-start.3 = (bf16[32,1024]{1,0:T(8,128)(2,1)S(1)}, bf16[32,1024]{1,0:T(8,128)(2,1)S(1)}, u32[]{:S(2)}, u32[]{:S(2)}) collective-permute-start(bf16[32,1024]{1,0:T(8,128)(2,1)S(1)} %maximum_select_fusion.1), channel_id=1, source_target_pairs={{0,8},{1,9},{2,10},{3,11},{4,12},{5,13},{6,14},{7,15},{8,0},{9,1},... | collective-permute-start | bytes 196616 | tf_op jit(solution)/shard_map/ppermute | solution.py:296
  32.1 0.8 %copy-start.2 = (bf16[128,256]{1,0:T(8,128)(2,1)S(1)}, bf16[128,256]{1,0:T(8,128)(2,1)}, u32[]{:S(2)}) copy-start(bf16[128,256]{1,0:T(8,128)(2,1)} %get-tuple-element.5) | copy-start | bytes 196612

commit v2 on v1

--- a/solution.py
+++ b/solution.py
@@ -179,6 +179,7 @@
 
 
 FUSED_ROWS = 128
+SUBLANES = 8
 
 
 def normalise(rows, scale_row, shift_row):
@@ -187,41 +188,52 @@
     return (centred * lax.rsqrt(variance + EPSILON) * scale_row + shift_row).astype(jnp.bfloat16)
 
 
+def received_at(at, seq_count, seq_local, res_local):
+    res_at, seq_at = at // seq_count, at % seq_count
+    return (seq_at // seq_local * res_local + res_at) * seq_local + seq_at % seq_local
+
+
+def sent_at(at, axis_size, seq_local, res_local):
+    group, own = at // seq_local, at % seq_local
+    return own * axis_size * res_local + group
+
+
+def pack_kernel(x_ref, order_ref, out_ref):
+    moved = jnp.dot(order_ref[...], x_ref[...], preferred_element_type=jnp.float32)
+    out_ref[...] = moved.astype(jnp.bfloat16)
+
+
 def column_kernel(
     x_ref,
     order_ref,
     live_ref,
-    factor_ref,
-    addend_ref,
+    vectors_ref,
     probe_ref,
     valve_ref,
-    valve_addend_ref,
     exit_ref,
-    exit_addend_ref,
-    stretch_ref,
-    shift_ref,
     twin_ref,
-    twin_shift_ref,
     expand_ref,
-    sum_ref,
     revised_ref,
     left_ref,
     right_ref,
     *,
     seq_count,
 ):
+    factor, addend, valve_addend, exit_addend, stretch, shift, twin_shift = (
+        vectors_ref[k : k + 1, :] for k in range(7)
+    )
     rows, width = x_ref.shape
     inner = HEAD_COUNT * HEAD_CHANNELS
     f32 = jnp.float32
     bf16 = jnp.bfloat16
     x = jnp.dot(order_ref[...], x_ref[...], preferred_element_type=f32)
-    normed = normalise(x, factor_ref[...], addend_ref[...])
+    normed = normalise(x, factor, addend)
     query_key = jnp.dot(normed, probe_ref[...], preferred_element_type=f32)
     value_gate = jnp.dot(normed, valve_ref[...], preferred_element_type=f32)
     query = (query_key[:, :inner] * HEAD_CHANNELS ** (-0.5)).astype(bf16)
     key = query_key[:, inner:].astype(bf16)
     value = value_gate[:, :inner].astype(bf16)
-    gating = jax.nn.sigmoid(value_gate[:, inner:] + valve_addend_ref[...])
+    gating = jax.nn.sigmoid(value_gate[:, inner:] + valve_addend)
     lane = lax.broadcasted_iota(jnp.int32, (rows, inner), 1)
     zero = jnp.zeros((rows, inner), bf16)
     heads = [
@@ -248,22 +260,25 @@
     weights = jnp.concatenate([weights[h] for h in range(HEAD_COUNT)], axis=1)
     attended = jnp.dot(weights, value_heads, preferred_element_type=f32)
     gated = (attended * gating).astype(bf16)
-    update = jnp.dot(gated, exit_ref[...], preferred_element_type=f32) + exit_addend_ref[...]
+    update = jnp.dot(gated, exit_ref[...], preferred_element_type=f32) + exit_addend
     revised = (x + update).astype(bf16)
     revised_ref[...] = revised
-    normed = normalise(revised.astype(f32), stretch_ref[...], shift_ref[...])
+    normed = normalise(revised.astype(f32), stretch, shift)
     projected = lax.dot_general(
         normed, twin_ref[...], (((1,), (1,)), ((), ())), preferred_element_type=f32
     )
     live_col = jnp.sum(jnp.where(row_at == col_at, live, 0.0), axis=1, keepdims=True)
-    projected = ((projected + twin_shift_ref[...]) * live_col).astype(bf16)
+    projected = ((projected + twin_shift[:, : 2 * OUTER_CHANNELS]) * live_col).astype(bf16)
     left_ref[...] = projected[:, :OUTER_CHANNELS]
     spread = jnp.dot(projected, expand_ref[...], preferred_element_type=f32)
     wide = spread.shape[1]
     seq_row = lax.broadcasted_iota(jnp.int32, (rows, wide), 0) & (seq_count - 1)
     seq_col = lax.broadcasted_iota(jnp.int32, (rows, wide), 1) & (seq_count - 1)
     spread = jnp.where(seq_row == seq_col, spread, 0.0).astype(bf16)
-    packed = jnp.dot(sum_ref[...], spread, preferred_element_type=f32)
+    part_row = lax.broadcasted_iota(jnp.int32, (SUBLANES, rows), 0) * seq_count
+    part_col = lax.broadcasted_iota(jnp.int32, (SUBLANES, rows), 1)
+    parts = (part_col >= part_row) & (part_col < part_row + seq_count)
+    packed = jnp.dot(parts.astype(bf16), spread, preferred_element_type=f32)
     right_ref[...] = packed[: right_ref.shape[0]].astype(bf16)
 
 
@@ -280,18 +295,27 @@
             ]
 
 
-def pair_kernel(right_ref, terms_ref, scale_ref, shift_ref, out_ref):
+def pair_kernel(right_ref, terms_ref, scale_ref, vectors_ref, out_ref):
+    shift = vectors_ref[7:8, :PAIR_DIM]
     result = jnp.dot(right_ref[...], terms_ref[...], preferred_element_type=jnp.float32)
     for i in range(out_ref.shape[0]):
         own = result[:, i * PAIR_DIM : (i + 1) * PAIR_DIM] * scale_ref[:, i : i + 1]
-        out_ref[i] = (own + shift_ref[...]).astype(jnp.bfloat16)
-
-
-def collect(block, axis_size, position):
+        out_ref[i] = (own + shift).astype(jnp.bfloat16)
+
+
+def held(*arrays):
+    return [pltpu.with_memory_space_constraint(a, pltpu.VMEM) for a in arrays]
+
+
+def collect(block, axis_size, position, beside):
     if axis_size & (axis_size - 1):
-        return lax.all_gather(block, "dap", axis=0, tiled=True)
+        return lax.all_gather(block, "dap", axis=0, tiled=True), beside
+    beside = list(beside)
     step = 1
     while step < axis_size:
+        due = len(beside) - (axis_size // step).bit_length() + 1
+        if 0 <= due < len(beside):
+            block, beside[due] = lax.optimization_barrier((block, beside[due]))
         pairs = [(j, j ^ step) for j in range(axis_size)]
         other = lax.ppermute(block, "dap", pairs)
         upper = (position & step) > 0
@@ -301,7 +325,7 @@
             jnp.concatenate([block, other], axis=0),
         )
         step *= 2
-    return block
+    return block, beside
 
 
 def fused_shards(
@@ -328,8 +352,19 @@
     seq_count = seq_local * axis_size
     rows = seq_count * res_local
     bf16 = jnp.bfloat16
-    sent = homolog_stack_tensor.reshape(seq_local, axis_size, res_local, width)
-    sent = jnp.transpose(sent, (1, 2, 0, 3)).reshape(axis_size, res_local * seq_local, width)
+    vmem = pl.BlockSpec(memory_space=pltpu.VMEM)
+    at = np.arange(rows)
+    pack_order = jnp.asarray(
+        sent_at(at, axis_size, seq_local, res_local)[:, None] == at[None, :], bf16
+    )
+    sent = pl.pallas_call(
+        pack_kernel,
+        out_shape=pltpu.VMEM((rows, width), bf16),
+        in_specs=[vmem] * 2,
+        out_specs=vmem,
+        name="pack",
+    )(homolog_stack_tensor.reshape(rows, width), pack_order)
+    sent = sent.reshape(axis_size, res_local * seq_local, width)
     got = lax.all_to_all(sent, "dap", split_axis=0, concat_axis=0, tiled=True)
     got = got.reshape(rows, width)
     position = lax.axis_index("dap")
@@ -343,50 +378,60 @@
         preferred_element_type=jnp.float32,
     )
     scale = 1.0 / jnp.maximum(counts, 1.0)
-    at = np.arange(rows)
-    res_at, seq_at = at // seq_count, at % seq_count
-    source = (seq_at // seq_local) * res_local * seq_local + res_at * seq_local + seq_at % seq_local
-    order = jnp.asarray(source[:, None] == at[None, :], bf16)
+    couple = couple_map_matrix.reshape(OUTER_CHANNELS, OUTER_CHANNELS * PAIR_DIM)
+    as_row = lambda v: jnp.pad(v.reshape(1, -1), ((0, 0), (0, width - v.shape[0])))
+    vectors = jnp.concatenate(
+        [
+            as_row(v)
+            for v in (
+                focus_normal_factor,
+                focus_normal_addend,
+                logistic_valve_addend,
+                focus_exit_addend,
+                product_mean_layer_stretch,
+                product_mean_layer_shift,
+                twin_map_shift,
+                couple_map_shift,
+            )
+        ]
+    )
+    got, live_row, scale, couple, vectors = lax.optimization_barrier(
+        (got, live_row, scale, couple, vectors)
+    )
+    order = jnp.asarray(
+        received_at(at, seq_count, seq_local, res_local)[:, None] == at[None, :], bf16
+    )
     wide = OUTER_CHANNELS * seq_count
     expand = jnp.asarray(
         np.arange(2 * OUTER_CHANNELS)[:, None] == OUTER_CHANNELS + np.arange(wide)[None, :] // seq_count,
         bf16,
     )
-    res_pad = -(-res_local // 8) * 8
-    summing = jnp.asarray(np.arange(res_pad)[:, None] == res_at[None, :], bf16)
-    as_row = lambda v: v.reshape(1, -1)
-    vmem = pl.BlockSpec(memory_space=pltpu.VMEM)
     revised, left, right = pl.pallas_call(
         lambda *refs: column_kernel(*refs, seq_count=seq_count),
         out_shape=(
-            jax.ShapeDtypeStruct((rows, width), bf16),
-            jax.ShapeDtypeStruct((rows, OUTER_CHANNELS), bf16),
-            jax.ShapeDtypeStruct((res_local, wide), bf16),
+            pltpu.VMEM((rows, width), bf16),
+            pltpu.VMEM((rows, OUTER_CHANNELS), bf16),
+            pltpu.VMEM((res_local, wide), bf16),
         ),
-        in_specs=[vmem] * 16,
+        in_specs=[vmem] * 9,
         out_specs=(vmem, vmem, vmem),
         name="column",
     )(
+      *held(
         got,
         order,
         live_row,
-        as_row(focus_normal_factor),
-        as_row(focus_normal_addend),
+        vectors,
         probe_index_weights,
         payload_valve_weights,
-        as_row(logistic_valve_addend),
         focus_exit_weights,
-        as_row(focus_exit_addend),
-        as_row(product_mean_layer_stretch),
-        as_row(product_mean_layer_shift),
         jnp.transpose(twin_map_matrix),
-        as_row(twin_map_shift),
         expand,
-        summing,
+      )
     )
     terms = pl.pallas_call(
         lambda *refs: left_kernel(*refs, seq_count=seq_count),
-        out_shape=jax.ShapeDtypeStruct((wide, res_local * PAIR_DIM), bf16),
+        out_shape=pltpu.VMEM((wide, res_local * PAIR_DIM), bf16),
         in_specs=[vmem] * 2,
         out_specs=vmem,
         cost_estimate=pl.CostEstimate(
@@ -395,16 +440,18 @@
             transcendentals=0,
         ),
         name="terms",
-    )(left, couple_map_matrix.reshape(OUTER_CHANNELS, OUTER_CHANNELS * PAIR_DIM))
+    )(*held(left, couple))
     alignment_after = jnp.transpose(revised.reshape(res_local, seq_count, width), (1, 0, 2))
-    right_all = collect(right, axis_size, position)
+    right_all, (alignment_after, terms) = collect(
+        right, axis_size, position, (alignment_after, terms)
+    )
     pair_rows = pl.pallas_call(
         pair_kernel,
         out_shape=jax.ShapeDtypeStruct((res_local, res_count, PAIR_DIM), bf16),
         in_specs=[vmem] * 4,
         out_specs=vmem,
         name="pairs",
-    )(right_all, terms, scale, as_row(couple_map_shift))
+    )(*held(right_all, terms, scale, vectors))
     return (alignment_after, pair_rows)
 
 

time: 39.8 us -> 34.4 us (0.86)
  Pallas kernels: 8.24 us -> 4.84 us
  waiting for transfers between devices: 15.3 us -> 17.7 us
  local copies, waits for them, and re-layouts: 4.46 us -> 2.09 us
  other arithmetic: 1.62 us -> 0.21 us
  matrix products: 0.81 us -> 0.2 us
    ppermute x4, waiting for transfers between devices: 9.32 us -> 12.7 us  [collect(): other = lax.ppermute(block, 'dap', pairs)]
    pallas_call x1, Pallas kernels: 2.34 us -> 0.41 us  [fused_shards(): pl.pallas_call(lambda *refs: left_kernel(*refs, seq_count=seq_count), out...]
    pallas_call x1, Pallas kernels: 3.74 us -> 1.87 us  [fused_shards(): pl.pallas_call(lambda *refs: column_kernel(*refs, seq_count=seq_count), o...]
    pallas_call x0 -> x1, Pallas kernels: none -> 1.63 us  [fused_shards(): pl.pallas_call(pack_kernel, out_shape=pltpu.VMEM((rows, width), bf16), in...]
    reshape x2 -> x0, local copies, waits for them, and re-layouts: 1.52 us -> none  [the longest x1 0.86 us: fused_shards(): sent = homolog_stack_tensor.reshape(seq_local, axis_size, res_local, width)]
    select_n x4, other arithmetic: 1.48 us -> 0.07 us  [collect(): jnp.where(upper, jnp.concatenate([other, block], axis=0), jnp.concatenate...]
    pallas_call x1, Pallas kernels: 2.16 us -> 0.93 us  [fused_shards(): pl.pallas_call(pair_kernel, out_shape=jax.ShapeDtypeStruct((res_local, re...]
    all_to_all x1, waiting for transfers between devices: 6.02 us -> 4.99 us  [fused_shards(): got = lax.all_to_all(sent, 'dap', split_axis=0, concat_axis=0, tiled=True)]
  transfers between devices with their start and end apart: 5 -> 5, of which waited for: 5 -> 5; matrix products, arithmetic and copies ran while one was open for 8% -> 7% of each run, Pallas kernels for 6% -> 1%
where the time goes in v2:
time: 34.4 us; the launch traced here: 34.1 us
  waiting for transfers between devices  17.7 us (51%)
  starting transfers between devices  8.23 us (24%)
  Pallas kernels  4.84 us (14%)
  local copies, waits for them, and re-layouts  2.09 us (6%)
  between operations  0.88 us (3%)
    ppermute x4, waiting for transfers between devices, collect(): other = lax.ppermute(block, 'dap', pairs)  12.7 us
    all_to_all x1, starting transfers between devices, fused_shards(): got = lax.all_to_all(sent, 'dap', split_axis=0, concat_axis=0, tiled=True)  7.55 us
    all_to_all x1, waiting for transfers between devices, fused_shards(): got = lax.all_to_all(sent, 'dap', split_axis=0, concat_axis=0, tiled=True)  4.99 us
    pallas_call x1, Pallas kernels, fused_shards(): pl.pallas_call(lambda *refs: column_kernel(*refs, seq_count=seq_count), o...  1.87 us
    pallas_call x1, Pallas kernels, fused_shards(): pl.pallas_call(pack_kernel, out_shape=pltpu.VMEM((rows, width), bf16), in...  1.63 us
    reshape x1, local copies, waits for them, and re-layouts, fused_shards(): couple_map_matrix.reshape(OUTER_CHANNELS, OUTER_CHANNELS * PAIR_DIM)  1.13 us
    pallas_call x1, Pallas kernels, fused_shards(): pl.pallas_call(pair_kernel, out_shape=jax.ShapeDtypeStruct((res_local, re...  0.93 us
  transfers between devices with their start and end apart: 5, of which 5 were waited for; matrix products, arithmetic and copies ran while one was open for 7% of the time, Pallas kernels for 1%

profile of v2, /device:TPU:0, one launch (start us, length us, event | category | flops | bytes accessed | tf_op | source)
XLA Modules:
  0.0 34.1 jit_solution(11922851156371116036)
XLA Ops:
  0.6 1.6 %pack.1 = bf16[128,256]{1,0:T(8,128)(2,1)} custom-call(bf16[128,256]{1,0:T(8,128)(2,1)} %bitcast.21, bf16[128,128]{1,0:T(8,128)(2,1)} %constant.26.clone.order_ref), custom_call_target="tpu_custom_call" | custom-call | tf_op jit(solution)/shard_map/pack/pallas_call | solution.py:360
  2.3 7.5 %all-to-all-start = ((bf16[16,8,256]{2,1,0:T(8,128)(2,1)}), bf16[16,8,256]{2,1,0:T(8,128)(2,1)S(1)}, u32[]{:S(2)}, u32[]{:S(2)}) async-start(bf16[16,8,256]{2,1,0:T(8,128)(2,1)} %bitcast.1), calls=%async_computation | async-start | bytes 131072 | tf_op jit(solution)/shard_map/all_to_all | solution.py:368
  9.9 0.1 broadcast_multiply_fusion
  9.9 0.1 convert_bitcast_fusion
  10.0 0.1 copy.21
  10.1 0.1 convert_element_type.29.refs_2_
  10.2 0.0 copy-start.10
  10.2 0.0 copy-start.11
  10.2 0.0 copy-start.1
  10.2 1.1 %reshape.61.refs_1_ = bf16[32,4096]{1,0:T(8,128)(2,1)S(1)} reshape(bf16[1024,128]{1,0:T(8,128)(2,1)} %param.33) | data formatting | bytes 524288 | tf_op jit(solution)/shard_map/reshape | solution.py:381
  11.5 0.2 fusion.scale_ref
  11.7 5.0 %all-to-all-done = bf16[16,8,256]{2,1,0:T(8,128)(2,1)S(1)} async-done(((bf16[16,8,256]{2,1,0:T(8,128)(2,1)}), bf16[16,8,256]{2,1,0:T(8,128)(2,1)S(1)}, u32[]{:S(2)}, u32[]{:S(2)}) %all-to-all-start) | async-done | bytes 65568 | tf_op jit(solution)/shard_map/all_to_all | solution.py:368
  16.8 1.9 %column.1 = (bf16[128,256]{1,0:T(8,128)(2,1)S(1)}, bf16[128,32]{1,0:T(8,128)(2,1)S(1)}, bf16[4,1024]{1,0:T(4,128)(2,1)S(1)}) custom-call(bf16[128,256]{1,0:T(8,128)(2,1)S(1)} %bitcast.18, bf16[128,128]{1,0:T(8,128)(2,1)S(1)} %copy-done.5, f32[1,128]{1,0:T(1,128)S(1)} %convert_element_type.29.refs_2_, f32[8,256]{1,0:T(8,128)S(1)} %concatenate.27.refs_3_.vectors_ref, ...), custom_call_target="tpu_custom_call" | custom-call | tf_op jit(solution)/shard_map/column/pallas_call | solution.py:409
  18.6 0.0 collective-permute-start
  18.7 1.2 %collective-permute-done = bf16[4,1024]{1,0:T(4,128)(2,1)S(1)} collective-permute-done((bf16[4,1024]{1,0:T(4,128)(2,1)S(1)}, bf16[4,1024]{1,0:T(4,128)(2,1)S(1)}, u32[]{:S(2)}, u32[]{:S(2)}) %collective-permute-start) | collective-permute-done | bytes 8224 | tf_op jit(solution)/shard_map/ppermute | solution.py:320
  19.9 0.2 collective-permute-start.1
  20.1 0.7 %copy.26 = bf16[4,32,256]{2,0,1:T(4,128)(2,1)} copy(bf16[4,32,256]{2,1,0:T(8,128)(2,1)S(1)} %bitcast.19) | data formatting | bytes 131072 | tf_op jit(solution)/shard_map/reshape | solution.py:444
  20.7 2.9 %collective-permute-done.1 = bf16[8,1024]{1,0:T(8,128)(2,1)S(1)} collective-permute-done((bf16[8,1024]{1,0:T(8,128)(2,1)S(1)}, bf16[8,1024]{1,0:T(8,128)(2,1)S(1)}, u32[]{:S(2)}, u32[]{:S(2)}) %collective-permute-start.1) | collective-permute-done | bytes 16416 | tf_op jit(solution)/shard_map/ppermute | solution.py:320
  23.7 0.2 collective-permute-start.2
  23.9 0.4 %terms.1.terms_ref = bf16[1024,512]{1,0:T(8,128)(2,1)S(1)} custom-call(bf16[128,32]{1,0:T(8,128)(2,1)S(1)} %get-tuple-element.21.refs_0_, bf16[32,4096]{1,0:T(8,128)(2,1)S(1)} %reshape.61.refs_1_), custom_call_target="tpu_custom_call" | custom-call | flops 67108864 | bytes 1048576 | tf_op jit(solution)/shard_map/terms/pallas_call | solution.py:432
  24.3 3.4 %collective-permute-done.2 = bf16[16,1024]{1,0:T(8,128)(2,1)S(1)} collective-permute-done((bf16[16,1024]{1,0:T(8,128)(2,1)S(1)}, bf16[16,1024]{1,0:T(8,128)(2,1)S(1)}, u32[]{:S(2)}, u32[]{:S(2)}) %collective-permute-start.2) | collective-permute-done | bytes 32800 | tf_op jit(solution)/shard_map/ppermute | solution.py:320
  27.7 0.3 collective-permute-start.3
  28.0 5.2 %collective-permute-done.3 = bf16[32,1024]{1,0:T(8,128)(2,1)S(1)} collective-permute-done((bf16[32,1024]{1,0:T(8,128)(2,1)S(1)}, bf16[32,1024]{1,0:T(8,128)(2,1)S(1)}, u32[]{:S(2)}, u32[]{:S(2)}) %collective-permute-start.3) | collective-permute-done | bytes 65568 | tf_op jit(solution)/shard_map/ppermute | solution.py:320
  33.2 0.9 %pairs.1 = bf16[4,64,128]{2,1,0:T(8,128)(2,1)} custom-call(bf16[64,1024]{1,0:T(8,128)(2,1)S(1)} %maximum_select_fusion.right_ref, bf16[1024,512]{1,0:T(8,128)(2,1)S(1)} %terms.1.terms_ref, f32[64,4]{1,0:T(8,128)S(1)} %fusion.scale_ref, f32[8,256]{1,0:T(8,128)S(1)} %concatenate.27.refs_3_.vectors_ref), custom_call_target="tpu_custom_call" | custom-call | tf_op jit(solution)/shard_map/pairs/pallas_call | solution.py:448
  (36 shorter events, 0.2 us)
Async XLA Ops:
  0.6 9.2 %copy-start.13 = (s32[32]{0:T(128)S(1)}, s32[32]{0:T(128)}, u32[]{:S(2)}) copy-start(s32[32]{0:T(128)} %param.21) | copy-start | bytes 388
  2.3 7.6 %copy-start.6 = (s32[32,64]{1,0:T(8,128)S(1)}, s32[32,64]{1,0:T(8,128)}, u32[]{:S(2)}) copy-start(s32[32,64]{1,0:T(8,128)} %param.20) | copy-start | bytes 24580
  2.3 14.5 %copy-start.3 = (bf16[64,1024]{1,0:T(8,128)(2,1)S(1)}, bf16[64,1024]{1,0:T(8,128)(2,1)}, u32[]{:S(2)}) copy-start(bf16[64,1024]{1,0:T(8,128)(2,1)} %constant.28.clone.refs_8_) | copy-start | bytes 393220
  2.3 14.4 %all-to-all-start = ((bf16[16,8,256]{2,1,0:T(8,128)(2,1)}), bf16[16,8,256]{2,1,0:T(8,128)(2,1)S(1)}, u32[]{:S(2)}, u32[]{:S(2)}) async-start(bf16[16,8,256]{2,1,0:T(8,128)(2,1)} %bitcast.1), calls=%async_computation | async-start | bytes 131072 | tf_op jit(solution)/shard_map/all_to_all | solution.py:368
  9.9 6.8 %copy-start.5 = (bf16[128,128]{1,0:T(8,128)(2,1)S(1)}, bf16[128,128]{1,0:T(8,128)(2,1)}, u32[]{:S(2)}) copy-start(bf16[128,128]{1,0:T(8,128)(2,1)} %constant.27.clone.refs_1_) | copy-start | bytes 98308
  10.0 1.4 %copy-start.14 = (f32[64]{0:T(128)S(1)}, f32[64]{0:T(128)}, u32[]{:S(2)}) copy-start(f32[64]{0:T(128)} %param.32) | copy-start | bytes 772
  10.0 1.4 %copy-start.15 = (f32[128]{0:T(128)S(1)}, f32[128]{0:T(128)}, u32[]{:S(2)}) copy-start(f32[128]{0:T(128)} %param.34) | copy-start | bytes 1540
  10.0 6.7 %copy-start.4 = (bf16[256,64]{0,1:T(8,128)(2,1)S(1)}, bf16[256,64]{0,1:T(8,128)(2,1)}, u32[]{:S(2)}) copy-start(bf16[256,64]{0,1:T(8,128)(2,1)} %param.31) | copy-start | bytes 98308
  10.2 1.3 %copy-start.7 = (f32[256]{0:T(256)S(1)}, f32[256]{0:T(256)}, u32[]{:S(2)}) copy-start(f32[256]{0:T(256)} %param.22) | copy-start | bytes 3076
  10.2 1.3 %copy-start.8 = (f32[256]{0:T(256)S(1)}, f32[256]{0:T(256)}, u32[]{:S(2)}) copy-start(f32[256]{0:T(256)} %param.23) | copy-start | bytes 3076
  10.2 1.3 %copy-start.9 = (f32[256]{0:T(256)S(1)}, f32[256]{0:T(256)}, u32[]{:S(2)}) copy-start(f32[256]{0:T(256)} %param.26) | copy-start | bytes 3076
  10.2 1.3 %copy-start.10 = (f32[256]{0:T(256)S(1)}, f32[256]{0:T(256)}, u32[]{:S(2)}) copy-start(f32[256]{0:T(256)} %param.28) | copy-start | bytes 3076
  10.2 1.3 %copy-start.11 = (f32[256]{0:T(256)S(1)}, f32[256]{0:T(256)}, u32[]{:S(2)}) copy-start(f32[256]{0:T(256)} %param.29) | copy-start | bytes 3076
  10.2 1.3 %copy-start.12 = (f32[256]{0:T(256)S(1)}, f32[256]{0:T(256)}, u32[]{:S(2)}) copy-start(f32[256]{0:T(256)} %param.30) | copy-start | bytes 3076
  10.2 6.5 %copy-start = (bf16[256,512]{1,0:T(8,128)(2,1)S(1)}, bf16[256,512]{1,0:T(8,128)(2,1)}, u32[]{:S(2)}) copy-start(bf16[256,512]{1,0:T(8,128)(2,1)} %refs_4_.1) | copy-start | bytes 786436
  10.2 6.5 %copy-start.1 = (bf16[256,512]{1,0:T(8,128)(2,1)S(1)}, bf16[256,512]{1,0:T(8,128)(2,1)}, u32[]{:S(2)}) copy-start(bf16[256,512]{1,0:T(8,128)(2,1)} %refs_5_.1) | copy-start | bytes 786436
  11.4 5.4 %copy-start.2 = (bf16[256,256]{1,0:T(8,128)(2,1)S(1)}, bf16[256,256]{1,0:T(8,128)(2,1)}, u32[]{:S(2)}) copy-start(bf16[256,256]{1,0:T(8,128)(2,1)} %refs_6_.1) | copy-start | bytes 393220
  18.6 1.2 %collective-permute-start = (bf16[4,1024]{1,0:T(4,128)(2,1)S(1)}, bf16[4,1024]{1,0:T(4,128)(2,1)S(1)}, u32[]{:S(2)}, u32[]{:S(2)}) collective-permute-start(bf16[4,1024]{1,0:T(4,128)(2,1)S(1)} %get-tuple-element.17), channel_id=1, source_target_pairs={{0,1},{1,0},{2,3},{3,2},{4,5},{5,4},{6,7},{7,6},{8,9},{9,8},{10,11... | collective-permute-start | bytes 24584 | tf_op jit(solution)/shard_map/ppermute | solution.py:320
  19.9 3.8 %collective-permute-start.1 = (bf16[8,1024]{1,0:T(8,128)(2,1)S(1)}, bf16[8,1024]{1,0:T(8,128)(2,1)S(1)}, u32[]{:S(2)}, u32[]{:S(2)}) collective-permute-start(bf16[8,1024]{1,0:T(8,128)(2,1)S(1)} %maximum_select_fusion.3), channel_id=1, source_target_pairs={{0,2},{1,3},{2,0},{3,1},{4,6},{5,7},{6,4},{7,5},{8,10},{9,11},{10,... | collective-permute-start | bytes 49160 | tf_op jit(solution)/shard_map/ppermute | solution.py:320
  23.7 4.0 %collective-permute-start.2 = (bf16[16,1024]{1,0:T(8,128)(2,1)S(1)}, bf16[16,1024]{1,0:T(8,128)(2,1)S(1)}, u32[]{:S(2)}, u32[]{:S(2)}) collective-permute-start(bf16[16,1024]{1,0:T(8,128)(2,1)S(1)} %maximum_select_fusion.2), channel_id=1, source_target_pairs={{0,4},{1,5},{2,6},{3,7},{4,0},{5,1},{6,2},{7,3},{8,12},{9,13},{10,... | collective-permute-start | bytes 98312 | tf_op jit(solution)/shard_map/ppermute | solution.py:320
  27.7 5.5 %collective-permute-start.3 = (bf16[32,1024]{1,0:T(8,128)(2,1)S(1)}, bf16[32,1024]{1,0:T(8,128)(2,1)S(1)}, u32[]{:S(2)}, u32[]{:S(2)}) collective-permute-start(bf16[32,1024]{1,0:T(8,128)(2,1)S(1)} %maximum_select_fusion.1), channel_id=1, source_target_pairs={{0,8},{1,9},{2,10},{3,11},{4,12},{5,13},{6,14},{7,15},{8,0},{9,1},... | collective-permute-start | bytes 196616 | tf_op jit(solution)/shard_map/ppermute | solution.py:320

commit v3 on v2

--- a/solution.py
+++ b/solution.py
@@ -295,9 +295,11 @@
             ]
 
 
-def pair_kernel(right_ref, terms_ref, scale_ref, vectors_ref, out_ref):
+def pair_kernel(right_ref, order_ref, terms_ref, scale_ref, vectors_ref, out_ref):
     shift = vectors_ref[7:8, :PAIR_DIM]
-    result = jnp.dot(right_ref[...], terms_ref[...], preferred_element_type=jnp.float32)
+    right = jnp.dot(order_ref[...], right_ref[...], preferred_element_type=jnp.float32)
+    right = right.astype(jnp.bfloat16)
+    result = jnp.dot(right, terms_ref[...], preferred_element_type=jnp.float32)
     for i in range(out_ref.shape[0]):
         own = result[:, i * PAIR_DIM : (i + 1) * PAIR_DIM] * scale_ref[:, i : i + 1]
         out_ref[i] = (own + shift).astype(jnp.bfloat16)
@@ -311,11 +313,10 @@
     if axis_size & (axis_size - 1):
         return lax.all_gather(block, "dap", axis=0, tiled=True), beside
     beside = list(beside)
-    step = 1
-    while step < axis_size:
-        due = len(beside) - (axis_size // step).bit_length() + 1
-        if 0 <= due < len(beside):
-            block, beside[due] = lax.optimization_barrier((block, beside[due]))
+    step, done = axis_size // 2, 0
+    while step:
+        if 0 < done <= len(beside):
+            block, beside[done - 1] = lax.optimization_barrier((block, beside[done - 1]))
         pairs = [(j, j ^ step) for j in range(axis_size)]
         other = lax.ppermute(block, "dap", pairs)
         upper = (position & step) > 0
@@ -324,8 +325,19 @@
             jnp.concatenate([other, block], axis=0),
             jnp.concatenate([block, other], axis=0),
         )
-        step *= 2
+        step, done = step // 2, done + 1
     return block, beside
+
+
+def collected_at(axis_size, part):
+    if axis_size & (axis_size - 1):
+        return np.arange(axis_size * part)
+    order = np.zeros(1, np.int64)
+    step = axis_size // 2
+    while step:
+        order = np.concatenate([order, order + step])
+        step //= 2
+    return (np.argsort(order)[:, None] * part + np.arange(part)).reshape(-1)
 
 
 def fused_shards(
@@ -445,13 +457,16 @@
     right_all, (alignment_after, terms) = collect(
         right, axis_size, position, (alignment_after, terms)
     )
+    pair_order = jnp.asarray(
+        collected_at(axis_size, res_local)[:, None] == np.arange(res_count)[None, :], bf16
+    )
     pair_rows = pl.pallas_call(
         pair_kernel,
         out_shape=jax.ShapeDtypeStruct((res_local, res_count, PAIR_DIM), bf16),
-        in_specs=[vmem] * 4,
+        in_specs=[vmem] * 5,
         out_specs=vmem,
         name="pairs",
-    )(*held(right_all, terms, scale, vectors))
+    )(*held(right_all, pair_order, terms, scale, vectors))
     return (alignment_after, pair_rows)
 
 

time: 34.4 us -> 33.7 us (0.980)
  waiting for transfers between devices: 17.7 us -> 16.9 us
    ppermute x4, waiting for transfers between devices: 12.7 us -> 11.9 us  [collect(): other = lax.ppermute(block, 'dap', pairs)]
where the time goes in v3:
time: 33.7 us; the launch traced here: 33.4 us
  waiting for transfers between devices  16.9 us (50%)
  starting transfers between devices  8.23 us (24%)
  Pallas kernels  4.94 us (15%)
  local copies, waits for them, and re-layouts  2.1 us (6%)
  between operations  0.9 us (3%)
    ppermute x4, waiting for transfers between devices, collect(): other = lax.ppermute(block, 'dap', pairs)  11.9 us
    all_to_all x1, starting transfers between devices, fused_shards(): got = lax.all_to_all(sent, 'dap', split_axis=0, concat_axis=0, tiled=True)  7.55 us
    all_to_all x1, waiting for transfers between devices, fused_shards(): got = lax.all_to_all(sent, 'dap', split_axis=0, concat_axis=0, tiled=True)  4.99 us
    pallas_call x1, Pallas kernels, fused_shards(): pl.pallas_call(lambda *refs: column_kernel(*refs, seq_count=seq_count), o...  1.87 us
    pallas_call x1, Pallas kernels, fused_shards(): pl.pallas_call(pack_kernel, out_shape=pltpu.VMEM((rows, width), bf16), in...  1.63 us
    reshape x1, local copies, waits for them, and re-layouts, fused_shards(): couple_map_matrix.reshape(OUTER_CHANNELS, OUTER_CHANNELS * PAIR_DIM)  1.13 us
    pallas_call x1, Pallas kernels, fused_shards(): pl.pallas_call(pair_kernel, out_shape=jax.ShapeDtypeStruct((res_local, re...  1.03 us
    ppermute x4, starting transfers between devices, collect(): other = lax.ppermute(block, 'dap', pairs)  0.69 us
  transfers between devices with their start and end apart: 5, of which 5 were waited for; matrix products, arithmetic and copies ran while one was open for 7% of the time, Pallas kernels for 1%

profile of v3, /device:TPU:0, one launch (start us, length us, event | category | flops | bytes accessed | tf_op | source)
XLA Modules:
  0.0 33.4 jit_solution(14040888306205859855)
XLA Ops:
  0.6 1.6 %pack.1 = bf16[128,256]{1,0:T(8,128)(2,1)} custom-call(bf16[128,256]{1,0:T(8,128)(2,1)} %bitcast.21, bf16[128,128]{1,0:T(8,128)(2,1)} %constant.28.clone.order_ref), custom_call_target="tpu_custom_call" | custom-call | tf_op jit(solution)/shard_map/pack/pallas_call | solution.py:372
  2.3 7.5 %all-to-all-start = ((bf16[16,8,256]{2,1,0:T(8,128)(2,1)}), bf16[16,8,256]{2,1,0:T(8,128)(2,1)S(1)}, u32[]{:S(2)}, u32[]{:S(2)}) async-start(bf16[16,8,256]{2,1,0:T(8,128)(2,1)} %bitcast.1), calls=%async_computation | async-start | bytes 131072 | tf_op jit(solution)/shard_map/all_to_all | solution.py:380
  9.9 0.1 broadcast_multiply_fusion
  9.9 0.1 convert_bitcast_fusion
  10.0 0.1 copy.22
  10.1 0.1 convert_element_type.29.refs_2_
  10.2 0.0 copy-start.11
  10.2 0.0 copy-start.12
  10.2 1.1 %reshape.61.refs_1_ = bf16[32,4096]{1,0:T(8,128)(2,1)S(1)} reshape(bf16[1024,128]{1,0:T(8,128)(2,1)} %param.34) | data formatting | bytes 524288 | tf_op jit(solution)/shard_map/reshape | solution.py:393
  11.5 0.2 fusion.scale_ref
  11.7 5.0 %all-to-all-done = bf16[16,8,256]{2,1,0:T(8,128)(2,1)S(1)} async-done(((bf16[16,8,256]{2,1,0:T(8,128)(2,1)}), bf16[16,8,256]{2,1,0:T(8,128)(2,1)S(1)}, u32[]{:S(2)}, u32[]{:S(2)}) %all-to-all-start) | async-done | bytes 65568 | tf_op jit(solution)/shard_map/all_to_all | solution.py:380
  16.8 1.9 %column.1 = (bf16[128,256]{1,0:T(8,128)(2,1)S(1)}, bf16[128,32]{1,0:T(8,128)(2,1)S(1)}, bf16[4,1024]{1,0:T(4,128)(2,1)S(1)}) custom-call(bf16[128,256]{1,0:T(8,128)(2,1)S(1)} %bitcast.18, bf16[128,128]{1,0:T(8,128)(2,1)S(1)} %copy-done.5, f32[1,128]{1,0:T(1,128)S(1)} %convert_element_type.29.refs_2_, f32[8,256]{1,0:T(8,128)S(1)} %concatenate.27.refs_3_.vectors_ref, ...), custom_call_target="tpu_custom_call" | custom-call | tf_op jit(solution)/shard_map/column/pallas_call | solution.py:421
  18.6 0.2 collective-permute-start
  18.9 0.7 %copy.27 = bf16[4,32,256]{2,0,1:T(4,128)(2,1)} copy(bf16[4,32,256]{2,1,0:T(8,128)(2,1)S(1)} %bitcast.19) | data formatting | bytes 131072 | tf_op jit(solution)/shard_map/reshape | solution.py:456
  19.6 3.7 %collective-permute-done = bf16[4,1024]{1,0:T(4,128)(2,1)S(1)} collective-permute-done((bf16[4,1024]{1,0:T(4,128)(2,1)S(1)}, bf16[4,1024]{1,0:T(4,128)(2,1)S(1)}, u32[]{:S(2)}, u32[]{:S(2)}) %collective-permute-start) | collective-permute-done | bytes 8224 | tf_op jit(solution)/shard_map/ppermute | solution.py:321
  23.2 0.2 collective-permute-start.1
  23.4 0.4 %terms.1.terms_ref = bf16[1024,512]{1,0:T(8,128)(2,1)S(1)} custom-call(bf16[128,32]{1,0:T(8,128)(2,1)S(1)} %get-tuple-element.21.refs_0_, bf16[32,4096]{1,0:T(8,128)(2,1)S(1)} %reshape.61.refs_1_), custom_call_target="tpu_custom_call" | custom-call | flops 67108864 | bytes 1048576 | tf_op jit(solution)/shard_map/terms/pallas_call | solution.py:444
  23.8 3.2 %collective-permute-done.1 = bf16[8,1024]{1,0:T(8,128)(2,1)S(1)} collective-permute-done((bf16[8,1024]{1,0:T(8,128)(2,1)S(1)}, bf16[8,1024]{1,0:T(8,128)(2,1)S(1)}, u32[]{:S(2)}, u32[]{:S(2)}) %collective-permute-start.1) | collective-permute-done | bytes 16416 | tf_op jit(solution)/shard_map/ppermute | solution.py:321
  27.1 0.2 collective-permute-start.2
  27.2 3.8 %collective-permute-done.2 = bf16[16,1024]{1,0:T(8,128)(2,1)S(1)} collective-permute-done((bf16[16,1024]{1,0:T(8,128)(2,1)S(1)}, bf16[16,1024]{1,0:T(8,128)(2,1)S(1)}, u32[]{:S(2)}, u32[]{:S(2)}) %collective-permute-start.2) | collective-permute-done | bytes 32800 | tf_op jit(solution)/shard_map/ppermute | solution.py:321
  31.1 0.1 collective-permute-start.3
  31.1 0.0 copy-start.6
  31.2 1.2 %collective-permute-done.3 = bf16[32,1024]{1,0:T(8,128)(2,1)S(1)} collective-permute-done((bf16[32,1024]{1,0:T(8,128)(2,1)S(1)}, bf16[32,1024]{1,0:T(8,128)(2,1)S(1)}, u32[]{:S(2)}, u32[]{:S(2)}) %collective-permute-start.3) | collective-permute-done | bytes 65568 | tf_op jit(solution)/shard_map/ppermute | solution.py:321
  32.4 1.0 %pairs.1 = bf16[4,64,128]{2,1,0:T(8,128)(2,1)} custom-call(bf16[64,1024]{1,0:T(8,128)(2,1)S(1)} %maximum_select_fusion.right_ref, bf16[64,64]{1,0:T(8,128)(2,1)S(1)} %copy-done.6, bf16[1024,512]{1,0:T(8,128)(2,1)S(1)} %terms.1.terms_ref, f32[64,4]{1,0:T(8,128)S(1)} %fusion.scale_ref, f32[8,256]{1,0:T(8,128)S(1)} %concatenate.27.refs_3_.vectors_ref), custom_call_target="tpu_custom_call" | custom-call | tf_op jit(solution)/shard_map/pairs/pallas_call | solution.py:463
  (38 shorter events, 0.2 us)
Async XLA Ops:
  0.6 9.2 %copy-start.14 = (s32[32]{0:T(128)S(1)}, s32[32]{0:T(128)}, u32[]{:S(2)}) copy-start(s32[32]{0:T(128)} %param.22) | copy-start | bytes 388
  2.3 7.6 %copy-start.7 = (s32[32,64]{1,0:T(8,128)S(1)}, s32[32,64]{1,0:T(8,128)}, u32[]{:S(2)}) copy-start(s32[32,64]{1,0:T(8,128)} %param.21) | copy-start | bytes 24580
  2.3 14.5 %copy-start.3 = (bf16[64,1024]{1,0:T(8,128)(2,1)S(1)}, bf16[64,1024]{1,0:T(8,128)(2,1)}, u32[]{:S(2)}) copy-start(bf16[64,1024]{1,0:T(8,128)(2,1)} %constant.30.clone.refs_8_) | copy-start | bytes 393220
  2.3 14.4 %all-to-all-start = ((bf16[16,8,256]{2,1,0:T(8,128)(2,1)}), bf16[16,8,256]{2,1,0:T(8,128)(2,1)S(1)}, u32[]{:S(2)}, u32[]{:S(2)}) async-start(bf16[16,8,256]{2,1,0:T(8,128)(2,1)} %bitcast.1), calls=%async_computation | async-start | bytes 131072 | tf_op jit(solution)/shard_map/all_to_all | solution.py:380
  9.9 6.8 %copy-start.5 = (bf16[128,128]{1,0:T(8,128)(2,1)S(1)}, bf16[128,128]{1,0:T(8,128)(2,1)}, u32[]{:S(2)}) copy-start(bf16[128,128]{1,0:T(8,128)(2,1)} %constant.29.clone.refs_1_) | copy-start | bytes 98308
  10.0 1.4 %copy-start.15 = (f32[64]{0:T(128)S(1)}, f32[64]{0:T(128)}, u32[]{:S(2)}) copy-start(f32[64]{0:T(128)} %param.33) | copy-start | bytes 772
  10.0 1.4 %copy-start.16 = (f32[128]{0:T(128)S(1)}, f32[128]{0:T(128)}, u32[]{:S(2)}) copy-start(f32[128]{0:T(128)} %param.35) | copy-start | bytes 1540
  10.0 6.7 %copy-start.4 = (bf16[256,64]{0,1:T(8,128)(2,1)S(1)}, bf16[256,64]{0,1:T(8,128)(2,1)}, u32[]{:S(2)}) copy-start(bf16[256,64]{0,1:T(8,128)(2,1)} %param.32) | copy-start | bytes 98308
  10.2 1.3 %copy-start.8 = (f32[256]{0:T(256)S(1)}, f32[256]{0:T(256)}, u32[]{:S(2)}) copy-start(f32[256]{0:T(256)} %param.23) | copy-start | bytes 3076
  10.2 1.3 %copy-start.9 = (f32[256]{0:T(256)S(1)}, f32[256]{0:T(256)}, u32[]{:S(2)}) copy-start(f32[256]{0:T(256)} %param.24) | copy-start | bytes 3076
  10.2 1.3 %copy-start.10 = (f32[256]{0:T(256)S(1)}, f32[256]{0:T(256)}, u32[]{:S(2)}) copy-start(f32[256]{0:T(256)} %param.27) | copy-start | bytes 3076
  10.2 1.3 %copy-start.11 = (f32[256]{0:T(256)S(1)}, f32[256]{0:T(256)}, u32[]{:S(2)}) copy-start(f32[256]{0:T(256)} %param.29) | copy-start | bytes 3076
  10.2 1.3 %copy-start.12 = (f32[256]{0:T(256)S(1)}, f32[256]{0:T(256)}, u32[]{:S(2)}) copy-start(f32[256]{0:T(256)} %param.30) | copy-start | bytes 3076
  10.2 1.3 %copy-start.13 = (f32[256]{0:T(256)S(1)}, f32[256]{0:T(256)}, u32[]{:S(2)}) copy-start(f32[256]{0:T(256)} %param.31) | copy-start | bytes 3076
  10.2 6.5 %copy-start = (bf16[256,512]{1,0:T(8,128)(2,1)S(1)}, bf16[256,512]{1,0:T(8,128)(2,1)}, u32[]{:S(2)}) copy-start(bf16[256,512]{1,0:T(8,128)(2,1)} %refs_4_.1) | copy-start | bytes 786436
  10.2 6.5 %copy-start.1 = (bf16[256,512]{1,0:T(8,128)(2,1)S(1)}, bf16[256,512]{1,0:T(8,128)(2,1)}, u32[]{:S(2)}) copy-start(bf16[256,512]{1,0:T(8,128)(2,1)} %refs_5_.1) | copy-start | bytes 786436
  11.4 5.4 %copy-start.2 = (bf16[256,256]{1,0:T(8,128)(2,1)S(1)}, bf16[256,256]{1,0:T(8,128)(2,1)}, u32[]{:S(2)}) copy-start(bf16[256,256]{1,0:T(8,128)(2,1)} %refs_6_.1) | copy-start | bytes 393220
  18.6 4.6 %collective-permute-start = (bf16[4,1024]{1,0:T(4,128)(2,1)S(1)}, bf16[4,1024]{1,0:T(4,128)(2,1)S(1)}, u32[]{:S(2)}, u32[]{:S(2)}) collective-permute-start(bf16[4,1024]{1,0:T(4,128)(2,1)S(1)} %get-tuple-element.17), channel_id=1, source_target_pairs={{0,8},{1,9},{2,10},{3,11},{4,12},{5,13},{6,14},{7,15},{8,0},{9,1},... | collective-permute-start | bytes 24584 | tf_op jit(solution)/shard_map/ppermute | solution.py:321
  23.2 3.8 %collective-permute-start.1 = (bf16[8,1024]{1,0:T(8,128)(2,1)S(1)}, bf16[8,1024]{1,0:T(8,128)(2,1)S(1)}, u32[]{:S(2)}, u32[]{:S(2)}) collective-permute-start(bf16[8,1024]{1,0:T(8,128)(2,1)S(1)} %maximum_select_fusion.3), channel_id=1, source_target_pairs={{0,4},{1,5},{2,6},{3,7},{4,0},{5,1},{6,2},{7,3},{8,12},{9,13},{10,... | collective-permute-start | bytes 49160 | tf_op jit(solution)/shard_map/ppermute | solution.py:321
  27.1 4.0 %collective-permute-start.2 = (bf16[16,1024]{1,0:T(8,128)(2,1)S(1)}, bf16[16,1024]{1,0:T(8,128)(2,1)S(1)}, u32[]{:S(2)}, u32[]{:S(2)}) collective-permute-start(bf16[16,1024]{1,0:T(8,128)(2,1)S(1)} %maximum_select_fusion.2), channel_id=1, source_target_pairs={{0,2},{1,3},{2,0},{3,1},{4,6},{5,7},{6,4},{7,5},{8,10},{9,11},{10,... | collective-permute-start | bytes 98312 | tf_op jit(solution)/shard_map/ppermute | solution.py:321
  31.1 1.3 %collective-permute-start.3 = (bf16[32,1024]{1,0:T(8,128)(2,1)S(1)}, bf16[32,1024]{1,0:T(8,128)(2,1)S(1)}, u32[]{:S(2)}, u32[]{:S(2)}) collective-permute-start(bf16[32,1024]{1,0:T(8,128)(2,1)S(1)} %maximum_select_fusion.1), channel_id=1, source_target_pairs={{0,1},{1,0},{2,3},{3,2},{4,5},{5,4},{6,7},{7,6},{8,9},{9,8},{10,11... | collective-permute-start | bytes 196616 | tf_op jit(solution)/shard_map/ppermute | solution.py:321
  31.1 1.3 %copy-start.6 = (bf16[64,64]{1,0:T(8,128)(2,1)S(1)}, bf16[64,64]{1,0:T(8,128)(2,1)}, u32[]{:S(2)}) copy-start(bf16[64,64]{1,0:T(8,128)(2,1)} %constant.31.clone.order_ref) | copy-start | bytes 24580
